TPU v7x, 32 devices: a whole 2x2x4 slice. The times are simulated.
32 devices in a mesh: dp: 8 (over y, x, core), mp: 4 (over z).
Axes of the slice: x: 2, y: 2, z: 4, core: 2. Of those that a mesh axis runs over, the one named last changes fastest.
Arguments:
- candidates: bfloat16 [64, 256, 768], P('dp', 'mp'), may hold values from -6 to 6
- owner_row: int32 [64], replicated, may hold values from 0 to 63, as said below
- selected: int32 [16], replicated, may hold values from 0 to 63, as said below
- dest_slot: int32 [16], replicated, may hold values from 0 to 15, as said below
- patch_weight: bfloat16 [768, 768], P(None, 'mp'), may hold values from -0.21875 to 0.21875
- positions: bfloat16 [256, 768], P(None, 'mp'), may hold values from -3 to 3
- qkv_weight: bfloat16 [768, 3, 768], P(None, None, 'mp'), may hold values from -1 to 1
- out_weight: bfloat16 [768, 768], P('mp'), may hold values from -0.21875 to 0.21875
- attn_gain: bfloat16 [768], replicated, may hold values from 0.099609375 to 1.8984375
- mlp_gain: bfloat16 [768], replicated, may hold values from 0.099609375 to 1.8984375
- up_weight: bfloat16 [768, 3072], P(None, 'mp'), may hold values from -0.21875 to 0.21875
- down_weight: bfloat16 [3072, 768], P('mp'), may hold values from -0.109375 to 0.109375
Outputs:
- layer_out: bfloat16 [16, 256, 768], P('dp', 'mp')
Inputs may be any that keep to these rules, and one draw needn't show every extreme that they name: `owner_row`: a permutation; storage row r sits on index r // 8 of dp. `selected`: distinct candidates; no index of dp stores more than 4 of them, and some index stores exactly 4. `dest_slot`: a permutation; the 2 slots s with equal s // 2 get candidates stored on different indices of dp.
All inputs are finite; a program needn't handle non-finite values.
Results may differ from a plain program's by a relative error of at most 0.012.
Values may be sent and summed in bfloat16 or wider, within the bound.
A program may use at most 128 MiB of HBM per device.

v0:
```python
import functools

import jax
import jax.numpy as jnp
from jax import lax
from jax.experimental import pallas as pl
from jax.experimental.pallas import tpu as pltpu
from jax.sharding import PartitionSpec as P

HEAD_DIM = 64
LANES = 128
PARTS = 2
MESH = pl.DeviceIdType.MESH
scope = jax.named_scope


def norm_rows(values, gain):
    average = jnp.mean(values, axis=-1, keepdims=True)
    centred = values - average
    variance = jnp.mean(centred * centred, axis=-1, keepdims=True)
    return centred * lax.rsqrt(variance + 1e-06) * gain


def dot(a, b):
    return jnp.dot(a, b, preferred_element_type=jnp.float32)


def dot_t(a, b):
    return lax.dot_general(a, b, (((1,), (1,)), ((), ())), preferred_element_type=jnp.float32)


def kernel(
    n_dp, n_mp, stored, per,
    owner_h, selected_h, dest_h,
    cand_h, pw, pos_t, gain1_h, gain2_h, qkv_h, out_h, up_h, down_h,
    out_hbm,
    owner_row, selected, dest_slot, gain1, gain2,
    cand, qkv, up, down, up2, down2, wrel, orel, posf,
    send, recv0, recv1, xr, n1, act, after, ctx, cx, n2, hid, part, ra, out,
    route_s, route_r, ws, wr, os_, or_, us, ur, ds_, dr, ag_s, ag_r, cx_s, cx_r, tk_s, tk_r, rs_s, rs_r, loc,
):
    dp = lax.axis_index("dp")
    mp = lax.axis_index("mp")
    recvs = (recv0, recv1)
    quarter, width = cand.shape[1], cand.shape[2]
    feats = pw.shape[0]
    rows = quarter // PARTS
    tokens = n_mp * quarter
    group = wrel.shape[2] // LANES
    side = mp + 1 - 2 * lax.rem(mp, 2)
    across = lax.rem(mp + n_mp // 2, n_mp)
    corner = n_mp - 1 - mp
    rel = (mp, side, across, corner)
    inner = (mp > 0) & (mp < n_mp - 1)
    outer = jnp.logical_not(inner)
    twin = dp + 1 - 2 * lax.rem(dp, 2)
    place = lax.rem(dp, group)
    first = dp - place

    barrier = pltpu.get_barrier_semaphore()
    for other in rel[1:]:
        pl.semaphore_signal(barrier, inc=1, device_id=(dp, other), device_id_type=MESH)

    @pl.loop(1, n_dp)
    def _(k):
        pl.semaphore_signal(barrier, inc=1, device_id=(lax.rem(dp + k, n_dp), mp), device_id_type=MESH)

    own_w = pltpu.make_async_copy(pw, wrel.at[0, :, pl.ds(0, width)], loc.at[0])
    own_p = pltpu.make_async_copy(pos_t, wrel.at[0, :, pl.ds(width, tokens)], loc.at[1])
    own_o = pltpu.make_async_copy(out_h, orel.at[0], loc.at[2])
    own_c = pltpu.make_async_copy(cand_h, cand, loc.at[3])
    tables = [
        pltpu.make_async_copy(src, dst, loc.at[7 + j])
        for j, (src, dst) in enumerate(
            ((owner_h, owner_row), (selected_h, selected), (dest_h, dest_slot), (gain1_h, gain1), (gain2_h, gain2))
        )
    ]
    for c in (*tables, own_c, own_w, own_p, own_o):
        c.start()
    later = [
        pltpu.make_async_copy(src, dst, loc.at[4 + j])
        for j, (src, dst) in enumerate(((qkv_h, qkv), (up_h, up), (down_h, down)))
    ]
    count = selected.shape[0]
    short = count <= 16

    def route(i):
        row = owner_row[selected[i]]
        slot = dest_slot[i]
        owner = lax.div(row, stored)
        return slot, owner, jnp.where(owner == dp, lax.div(slot, per), -1), lax.rem(row, stored)

    for c in tables:
        c.wait()
    routes = [route(i) for i in range(count)] if short else []

    def choose(key, value, wanted):
        if short:
            found = jnp.int32(0)
            for entry in routes:
                found = jnp.where(entry[key] == wanted, entry[value], found)
            return found

        def body(i, found):
            entry = route(i)
            return jnp.where(entry[key] == wanted, entry[value], found)
        return lax.fori_loop(0, count, body, jnp.int32(0))

    def remote(src, dst, ss, rs, where):
        return pltpu.make_async_remote_copy(
            src_ref=src, dst_ref=dst, send_sem=ss, recv_sem=rs, device_id=where, device_id_type=MESH
        )

    def flip(index, bit):
        return index + bit - 2 * bit * lax.rem(lax.div(index, bit), 2)

    def w_cut(j):
        return pl.ds(0, feats), pl.ds(pl.multiple_of(j * LANES, LANES), LANES)

    o_rows, o_cols = 2 * feats // group, width // 2

    def o_cut(j):
        return (
            pl.ds(pl.multiple_of(lax.div(j, 2) * o_rows, o_rows), o_rows),
            pl.ds(pl.multiple_of(lax.rem(j, 2) * o_cols, o_cols), o_cols),
        )

    core = lax.rem(place, 2)
    along_x, along_y = flip(place, 2), flip(place, 4)
    peers = (
        along_y + core * (along_x - along_y), along_x + core * (along_y - along_x), flip(along_x, 4)
    )
    homes = [first + peer for peer in peers]

    def landed(ref, sem):
        remote(ref, ref, sem, sem, (twin, mp)).wait_recv()

    def left(ref, sem):
        remote(ref, ref, sem, sem, (twin, mp)).wait_send()

    class Spread:
        def __init__(self, buf, cut, several, ss, rs, lead):
            self.buf, self.cut, self.several, self.ss, self.rs, self.lead = buf, cut, several, ss, rs, lead

        def block(self, j):
            return self.buf.at[(*self.lead, *self.cut(j))]

        def group(self, n):
            return self.buf.at[(*self.lead, *self.several(n))]

        def over_xy(self, direct=False):
            mine = self.block(place)
            for k in (2, 0, 1) if direct else (0, 1):
                remote(mine, mine, self.ss.at[1], self.rs.at[min(1 + k, 2)], (homes[k], mp)).start()
            remote(mine, mine, self.ss.at[2], self.rs.at[3], (twin, mp)).start()

        def to_twin(self, j):
            got = self.block(j)
            remote(got, got, self.ss.at[2], self.rs.at[3], (twin, mp)).start()

        def relay(self):
            got = self.block(peers[0])
            landed(got, self.rs.at[1])
            remote(got, got, self.ss.at[1], self.rs.at[2], (homes[1], mp)).start()
            self.to_twin(peers[0])

        def near(self):
            landed(self.block(peers[0]), self.rs.at[1])
            self.to_twin(peers[0])

        def rest(self):
            landed(self.group(2), self.rs.at[2])
            self.to_twin(peers[1])
            self.to_twin(peers[2])

        def end(self):
            landed(self.group(4), self.rs.at[3])

        def drain(self):
            left(self.group(3), self.ss.at[1])
            left(self.group(4), self.ss.at[2])

    class Planes(Spread):
        def over_z(self):
            cut = self.cut(place)
            for r in (2, 3, 1):
                remote(
                    self.buf.at[(0, *cut)], self.buf.at[(r, *cut)], self.ss.at[0], self.rs.at[0], (dp, rel[r])
                ).start()

        def from_z(self):
            landed(self.block(place), self.rs.at[0])

        def z_left(self, n):
            left(self.block(place), self.ss.at[0])

    class Lend(Spread):
        def over_z(self, src):
            rows_ = self.cut(place)
            remote(src.at[rows_], self.buf.at[rows_], self.ss.at[0], self.rs.at[0], (dp, side)).start()

        def from_z(self):
            landed(self.block(place), self.rs.at[0])

    class Inner(Planes):
        def over_z(self):
            cut = self.cut(place)

            def send_to(r):
                remote(
                    self.buf.at[(0, *cut)], self.buf.at[(r, *cut)], self.ss.at[0], self.rs.at[0], (dp, rel[r])
                ).start()

            @pl.when(outer)
            def _():
                send_to(2)
                send_to(1)

            @pl.when(inner)
            def _():
                send_to(3)

        def z_left(self, n):
            cut = self.cut(place)
            left(self.buf.at[(pl.ds(0, n), *cut)], self.ss.at[0])

    def w_several(n):
        return pl.ds(0, feats), pl.ds(0, n * LANES)

    def o_several(n):
        return pl.ds(0, n * o_rows), pl.ds(0, o_cols)

    l_rows = up.shape[0] // group

    def l_cut(j):
        return (pl.ds(pl.multiple_of(j * l_rows, l_rows), l_rows),)

    def l_several(n):
        return (pl.ds(0, n * l_rows),)

    others = (pl.ds(1, n_mp - 1),)
    spread_w = Planes(wrel, w_cut, w_several, ws, wr, others)
    spread_o = Inner(orel, o_cut, o_several, os_, or_, others)
    lend_up = Lend(up2, l_cut, l_several, us, ur, ())
    lend_down = Lend(down2, l_cut, l_several, ds_, dr, ())

    for c in (own_w, own_p, own_c, own_o):
        c.wait()
    with scope("s_barrier"):
        pl.semaphore_wait(barrier, n_mp - 1 + n_dp - 1)

    with scope("s_pass"):
        spread_w.over_z()

        @pl.when(outer)
        def _():
            lend_up.over_z(up_h)
        spread_o.over_z()
        learners = []
        if short:
            learners = [lax.rem(dp + k, n_dp) for k in range(1, n_dp)]
        if n_dp == group:
            learners = [flip(home, b) if b else home for home in homes[::-1] for b in (0, 1)] + [twin]
        for h in range(PARTS):
            def pass_on(k):
                learner = k if short else lax.rem(dp + n_dp - k, n_dp)
                send[h, learner] = cand[choose(2, 3, learner), h * rows:(h + 1) * rows]
                remote(
                    send.at[h, learner], recvs[h].at[dp], route_s.at[h], route_r.at[h], (learner, mp)
                ).start()

            if short:
                for learner in learners:
                    pass_on(learner)
            else:
                pl.loop(1, n_dp)(pass_on)
            recvs[h][dp] = cand[choose(2, 3, dp), h * rows:(h + 1) * rows]
        for c in later:
            c.start()
        senders = [choose(0, 1, dp * per + e) for e in range(per)]

    every = range(per)
    halves = range(PARTS)
    chunks = [(e, h) for h in halves for e in every]

    def copy(src, dst, ss, rs, where):
        remote(src, dst, ss, rs, where).start()

    def gather_send(e, h, src, r, where):
        at = 3 * (e * PARTS + h) + r - 1
        copy(xr.at[e, h, src], xr.at[e, h, r], ag_s.at[0], ag_r.at[at], (dp, where))

    def gather_land(e, h, r):
        landed(xr.at[e, h, r], ag_r.at[3 * (e * PARTS + h) + r - 1])

    def gather_start(e, h):
        @pl.when(outer)
        def _():
            gather_send(e, h, 0, 2, across)

        @pl.when(inner)
        def _():
            gather_send(e, h, 0, 3, corner)
        gather_send(e, h, 0, 1, side)

    def gather_forward(e, h):
        @pl.when(inner)
        def _():
            gather_land(e, h, 3)
            gather_send(e, h, 3, 2, side)
            gather_land(e, h, 2)
            gather_send(e, h, 2, 3, side)

    def gather_end(e, h):
        @pl.when(outer)
        def _():
            gather_land(e, h, 2)
            gather_land(e, h, 3)
        gather_land(e, h, 1)

    def take(h):
        landed(recvs[h].at[pl.ds(0, n_dp - 1)], route_r.at[h])
        for e in every:
            xr[e, h, 0] = recvs[h][senders[e]]
            gather_start(e, h)

    def on_inner(name, *calls):
        with scope(name):
            @pl.when(inner)
            def _():
                for call in calls:
                    call()

    with scope("s_route0"):
        take(0)
    with scope("s_wxy"):
        spread_w.from_z()
        spread_w.over_xy()
    with scope("s_route1"):
        take(1)

        @pl.when(outer)
        def _():
            lend_down.over_z(down_h)
    with scope("s_wrelay"):
        spread_w.relay()
    for e in every:
        with scope("s_fwd1a"):
            gather_forward(e, 0)
    on_inner("s_oxy", spread_o.from_z, spread_o.over_xy)
    with scope("s_fwd1b"):
        gather_forward(0, PARTS - 1)
    with scope("s_wrest"):
        spread_w.rest()
    with scope("s_fwd1b"):
        gather_forward(1, PARTS - 1)
    on_inner("s_upxy", lend_up.from_z, lend_up.over_xy)
    with scope("s_wend"):
        spread_w.end()
    with scope("s_pos"):
        for q in range(n_mp):
            posf[:, q * feats:(q + 1) * feats] = jnp.transpose(wrel[rel[q], :, width:].astype(jnp.float32))

    g1 = gain1[...].astype(jnp.float32).reshape(1, width)
    g2 = gain2[...].astype(jnp.float32).reshape(1, width)

    def embed(those, h):
        w = jnp.concatenate([wrel[rel[q], :, :width] for q in range(n_mp)], axis=0)
        pos = jnp.concatenate(
            [posf[pl.ds(pl.multiple_of(rel[r] * quarter + h * rows, rows), rows)] for r in range(n_mp)], axis=0
        )
        size = n_mp * rows
        x = jnp.concatenate([xr[e, h].reshape(size, width) for e in those], axis=0)
        prod = dot_t(x, w)
        for j, e in enumerate(those):
            value = (prod[j * size:(j + 1) * size] + pos).astype(jnp.bfloat16).astype(jnp.float32)
            act[e, h] = value[:2 * rows].reshape(2, rows, width)
            n1[e, h * size:(h + 1) * size] = norm_rows(value, g1).astype(jnp.bfloat16)

    def attend(e):
        qkv_all = dot_t(n1[e], qkv[...].reshape(3 * feats, width)).astype(jnp.bfloat16)
        q = qkv_all[:, :feats] * jnp.bfloat16(HEAD_DIM ** (-0.5))
        k = qkv_all[:, feats:2 * feats]
        v = qkv_all[:, 2 * feats:]
        for head in range(feats // HEAD_DIM):
            cut = slice(head * HEAD_DIM, (head + 1) * HEAD_DIM)
            s = dot_t(q[:, cut], k[:, cut])
            p = jnp.exp(s - jnp.max(s, axis=-1, keepdims=True))
            total = jnp.sum(p, axis=-1, keepdims=True)
            c = (dot(p.astype(jnp.bfloat16), v[:, cut]) / total).astype(jnp.bfloat16)
            c = c.reshape(PARTS, n_mp, rows, HEAD_DIM)
            for h in halves:
                at = h * feats + head * HEAD_DIM
                ctx[e, :, :, at:at + HEAD_DIM] = c[h]
        def send_to(r, at, b, where):
            copy(ctx.at[e, r], cx.at[e, at, b], cx_s.at[0], cx_r.at[e], (dp, where))

        @pl.when(outer)
        def _():
            for r in (2, 3):
                send_to(r, 1, r - 2, across)
            for r in (0, 1):
                send_to(r, 0, 1 - r, side)

        @pl.when(inner)
        def _():
            for r in (3, 2):
                send_to(r, 2, 3 - r, corner)

    def context_land(e):
        landed(cx.at[e], cx_r.at[e])

    def project(e):
        total = jnp.zeros((2 * quarter, width), jnp.float32)
        for r in range(n_mp):
            packed = [ctx[e, b] if r == 0 else cx[e, r - 1, b] for b in range(2)]
            block = jnp.concatenate(
                [packed[b][:, h * feats:(h + 1) * feats] for h in halves for b in range(2)], axis=0
            )
            total += dot(block, orel[r])
        value = act[e].reshape(2 * quarter, width) + total
        after[e] = value.reshape(PARTS, 2, rows, width)
        normed = norm_rows(value, g2).astype(jnp.bfloat16).reshape(PARTS, 2, rows, width)
        for h in halves:
            at = tk_r.at[e * PARTS + h]
            for b in range(2):
                n2[e, h, b] = normed[h, b]
                copy(n2.at[e, h, b], n2.at[e, h, 3 - b], tk_s.at[0], at, (dp, corner))

    def mlp_up(e, h):
        landed(n2.at[e, h, pl.ds(2, 2)], tk_r.at[e * PARTS + h])
        x = n2[e, h].reshape(n_mp * rows, width)
        for j, u in enumerate((up, up2)):
            y = dot(x, u[...])
            hid[e, h, j] = (0.5 * y * (1.0 + lax.erf(y * 0.7071067811865476))).astype(jnp.bfloat16)

    def mlp_down(e, h):
        total = dot(hid[e, h, 0], down[...]) + dot(hid[e, h, 1], down2[...])
        total = total.reshape(n_mp, rows, width)
        for r in (2, 3, 1, 0):
            part[e, h, r] = (total[r] + after[e, h, r] if r < 2 else total[r]).astype(jnp.bfloat16)
        for r in (2, 3, 1):
            copy(part.at[e, h, r], ra.at[e, h, int(r > 1)], rs_s.at[0], rs_r.at[e * PARTS + h], (dp, rel[r]))

    def finish(e, h, mine):
        got = pl.ds(0, 2) if mine is None else pl.ds(1, 1)
        landed(ra.at[e, h, got], rs_r.at[e * PARTS + h])
        total = (ra[e, h, 0] if mine is None else mine[e, h, 0]).astype(jnp.float32) + ra[e, h, 1].astype(jnp.float32)
        out[e, h] = total.astype(jnp.bfloat16)
        pltpu.make_async_copy(out.at[e, h], out_hbm.at[e, pl.ds(h * rows, rows)], loc.at[0]).start()

    with scope("s_ag1end"):
        for e in every:
            gather_end(e, 0)
    with scope("s_embed"):
        embed(every, 0)
    for e in every:
        with scope("s_ag1end"):
            gather_end(e, 1)
        with scope("s_embed"):
            embed([e], 1)
        if e == 0:
            later[0].wait()
        with scope("s_attend"):
            attend(e)
        if e == 0:
            on_inner("s_orelay", spread_o.relay)
            on_inner("s_uprelay", lend_up.relay)
            on_inner("s_downxy", lend_down.from_z, lend_down.over_xy)
    on_inner("s_orest", spread_o.rest)
    on_inner("s_oend", spread_o.end)
    for e in every:
        on_inner("s_cwait", functools.partial(context_land, e))
        on_inner("s_proj", functools.partial(project, e))
        if e == 0:
            on_inner("s_downrelay", lend_down.relay)
    for c in later[1:]:
        c.wait()

    @pl.when(inner)
    def _():
        with scope("s_uprest"):
            lend_up.rest()
        with scope("s_downrest"):
            lend_down.rest()
        with scope("s_upend"):
            lend_up.end()
        with scope("s_downend"):
            lend_down.end()
        for e, h in [(e, h) for e in every for h in halves][0:]:
            with scope("s_mlpup"):
                mlp_up(e, h)
            with scope("s_mlp"):
                mlp_down(e, h)
        with scope("s_finish"):
            for e in every:
                for h in halves:
                    finish(e, h, part)

    @pl.when(outer)
    def _():
        with scope("s_finish"):
            for e in every:
                for h in halves:
                    finish(e, h, None)

    with scope("s_drain"):
        for h in halves:
            left(send.at[h, pl.ds(0, n_dp - 1)], route_s.at[h])
        spread_w.z_left(3)
        spread_w.drain()

        @pl.when(inner)
        def _():
            spread_o.z_left(1)
            spread_o.drain()
            lend_up.drain()
            lend_down.drain()
            left(xr, ag_s.at[0])
            left(ctx.at[0], cx_s.at[0])
            left(n2.at[0], tk_s.at[0])
            left(part.at[:, :, pl.ds(0, n_mp - 1)], rs_s.at[0])

        @pl.when(outer)
        def _():
            spread_o.z_left(2)
            left(lend_up.block(place), us.at[0])
            left(lend_down.block(place), ds_.at[0])
            left(xr.at[0], ag_s.at[0])
            left(ctx, cx_s.at[0])

        pltpu.make_async_copy(out, out, loc.at[0]).wait()


def solution(mesh):
    n_dp, n_mp = mesh.shape["dp"], mesh.shape["mp"]

    def local(
        candidates, owner_row, selected, dest_slot, patch_weight, positions,
        qkv_weight, out_weight, attn_gain, mlp_gain, up_weight, down_weight,
    ):
        stored, quarter, width = candidates.shape
        per = selected.shape[0] // n_dp
        feats = patch_weight.shape[1]
        tokens = positions.shape[0]
        rows = quarter // PARTS
        qkv = jnp.transpose(qkv_weight, (1, 2, 0))
        hb = pl.BlockSpec(memory_space=pl.ANY)
        bf, f32 = jnp.bfloat16, jnp.float32
        dma = pltpu.SemaphoreType.DMA
        chunks = per * PARTS
        return pl.pallas_call(
            functools.partial(kernel, n_dp, n_mp, stored, per),
            out_shape=jax.ShapeDtypeStruct((per, quarter, width), bf),
            in_specs=[hb] * 12,
            out_specs=hb,
            scratch_shapes=[
                *[pltpu.SMEM(x.shape, x.dtype) for x in (owner_row, selected, dest_slot)],
                pltpu.VMEM(attn_gain.shape, bf), pltpu.VMEM(mlp_gain.shape, bf),
                pltpu.VMEM(candidates.shape, bf), pltpu.VMEM(qkv.shape, bf),
                pltpu.VMEM(up_weight.shape, bf), pltpu.VMEM(down_weight.shape, bf),
                pltpu.VMEM(up_weight.shape, bf), pltpu.VMEM(down_weight.shape, bf),
                pltpu.VMEM((n_mp, feats, width + tokens), bf),
                pltpu.VMEM((n_mp, feats, width), bf),
                pltpu.VMEM((tokens, width), f32),
                pltpu.VMEM((PARTS, n_dp, rows, width), bf),
                pltpu.VMEM((n_dp, rows, width), bf), pltpu.VMEM((n_dp, rows, width), bf),
                pltpu.VMEM((per, PARTS, n_mp, rows, width), bf),
                pltpu.VMEM((per, tokens, width), bf),
                pltpu.VMEM((per, PARTS, 2, rows, width), f32),
                pltpu.VMEM((per, PARTS, 2, rows, width), f32),
                pltpu.VMEM((per, n_mp, rows, PARTS * feats), bf),
                pltpu.VMEM((per, n_mp - 1, 2, rows, PARTS * feats), bf),
                pltpu.VMEM((per, PARTS, n_mp, rows, width), bf),
                pltpu.VMEM((per, PARTS, 2, n_mp * rows, up_weight.shape[1]), bf),
                pltpu.VMEM((per, PARTS, n_mp, rows, width), bf),
                pltpu.VMEM((per, PARTS, 2, rows, width), bf),
                pltpu.VMEM((per, PARTS, rows, width), bf),
                *[dma((n,)) for n in (PARTS, PARTS, 3, 4, 3, 4, 3, 4, 3, 4)],
                *[dma((n,)) for n in (1, 3 * chunks, 1, per, 1, chunks, 1, chunks, 12)],
            ],
            compiler_params=pltpu.CompilerParams(
                collective_id=0, has_side_effects=True, vmem_limit_bytes=60 * 1024 * 1024
            ),
        )(
            owner_row, selected, dest_slot, candidates, patch_weight.T, positions.T,
            attn_gain, mlp_gain, qkv, out_weight, up_weight, down_weight,
        )

    return jax.shard_map(
        local,
        mesh=mesh,
        in_specs=(
            P("dp", "mp", None), P(), P(), P(), P(None, "mp"), P(None, "mp"), P(None, None, "mp"),
            P("mp", None), P(), P(), P(None, "mp"), P("mp", None),
        ),
        out_specs=P("dp", "mp", None),
        check_vma=False,
    )
```

profile of v0, /device:TPU:0, one launch (start us, length us, event | category | flops | bytes accessed | tf_op | source)
XLA Modules:
  0.0 53.9 jit_solution(617242209376843004)
XLA Ops:
  0.0 52.3 %shard_map.118 = bf16[2,64,768]{2,1,0:T(8,128)(2,1)} custom-call(s32[64]{0:T(128)} %owner_h.1, s32[16]{0:T(128)} %selected_h.1, s32[16]{0:T(128)} %dest_h.1, bf16[8,64,768]{2,1,0:T(8,128)(2,1)} %cand_h.1, bf16[192,768]{1,0:T(8,128)(2,1)} %bitcast.4, bf16[192,256]{1,0:T(8,128)(2,1)} %bitcast.5, bf16[768]{0:T(1024)(128)(2,1)} %gain1_h.1, ...), custom_call_target="tpu_custom_call" | custom-call | tf_op jit(solution)/shard_map/pallas_call | solution.py:552
  52.3 1.6 %copy.14 = bf16[2,64,768]{2,1,0:T(8,128)(2,1)} copy(bf16[2,64,768]{2,1,0:T(8,128)(2,1)} %shard_map.118) | data formatting | bytes 393216
where the time goes:
time: 54.1 us; the launch traced here: 53.9 us
  Pallas kernels  52.3 us (97%)
  local copies, waits for them, and re-layouts  1.62 us (3%)
    pallas_call x1, Pallas kernels, local(): pl.pallas_call(functools.partial(kernel, n_dp, n_mp, stored, per), out_sh...  52.3 us
    unnamed x1, local copies, waits for them, and re-layouts  1.62 us

commit v1 on v0

--- a/solution.py
+++ b/solution.py
@@ -461,12 +461,12 @@
             embed([e], 1)
         if e == 0:
             later[0].wait()
+            on_inner("s_orelay", spread_o.relay)
+            on_inner("s_downxy", lend_down.from_z, lend_down.over_xy)
         with scope("s_attend"):
             attend(e)
         if e == 0:
-            on_inner("s_orelay", spread_o.relay)
             on_inner("s_uprelay", lend_up.relay)
-            on_inner("s_downxy", lend_down.from_z, lend_down.over_xy)
     on_inner("s_orest", spread_o.rest)
     on_inner("s_oend", spread_o.end)
     for e in every:

time: 54.1 us -> 54 us (level)
  no operation moved by 1% of the time
where the time goes in v1:
time: 54 us; the launch traced here: 53.8 us
  Pallas kernels  52.2 us (97%)
  local copies, waits for them, and re-layouts  1.62 us (3%)
    pallas_call x1, Pallas kernels, local(): pl.pallas_call(functools.partial(kernel, n_dp, n_mp, stored, per), out_sh...  52.2 us
    unnamed x1, local copies, waits for them, and re-layouts  1.62 us

profile of v1, /device:TPU:0, one launch (start us, length us, event | category | flops | bytes accessed | tf_op | source)
XLA Modules:
  0.0 53.8 jit_solution(3662468859762963464)
XLA Ops:
  0.0 52.2 %shard_map.118 = bf16[2,64,768]{2,1,0:T(8,128)(2,1)} custom-call(s32[64]{0:T(128)} %owner_h.1, s32[16]{0:T(128)} %selected_h.1, s32[16]{0:T(128)} %dest_h.1, bf16[8,64,768]{2,1,0:T(8,128)(2,1)} %cand_h.1, bf16[192,768]{1,0:T(8,128)(2,1)} %bitcast.4, bf16[192,256]{1,0:T(8,128)(2,1)} %bitcast.5, bf16[768]{0:T(1024)(128)(2,1)} %gain1_h.1, ...), custom_call_target="tpu_custom_call" | custom-call | tf_op jit(solution)/shard_map/pallas_call | solution.py:552
  52.2 1.6 %copy.14 = bf16[2,64,768]{2,1,0:T(8,128)(2,1)} copy(bf16[2,64,768]{2,1,0:T(8,128)(2,1)} %shard_map.118) | data formatting | bytes 393216
